TPU v7x, 32 devices: a whole 2x2x4 slice. The times are simulated.
32 devices in a mesh: ep: 8 (over z, y), dp: 4 (over x, core).
Axes of the slice: x: 2, y: 2, z: 4, core: 2. Of those that a mesh axis runs over, the one named last changes fastest.
Arguments:
- tokens: bfloat16 [6144, 2880], P(('ep', 'dp')), may hold values from -64 to 64
- out_grad: bfloat16 [6144, 2880], P(('ep', 'dp')), may hold values from -6 to 6
- indices: int32 [6144, 4], P(('ep', 'dp')), may hold values from 0 to 31, as said below
- expert_rows: bfloat16 [4, 32, 8, 36, 2880], P('dp', 'ep'), may hold values from -0.111328125 to 0.111328125
- router_weight: bfloat16 [2880, 32], replicated, may hold values from -1 to 1
- router_bias: float32 [32], replicated, may hold values from -3 to 3
- balance_scale: float32 [1], replicated, may hold values from 64 to 256
Outputs:
- token_grad: bfloat16 [6144, 2880], P(('ep', 'dp'))
- weight_grad: float32 [2880, 32], P('dp', 'ep')
- balance_loss: float32 [1], replicated
Inputs may be any that keep to these rules, and one draw needn't show every extreme that they name: `indices`: each row names 4 different experts. Within the 192 rows of one device no expert is named by more than 36 rows, and some expert is named by exactly 36 rows. Within the rows of one device the 4 experts of one ep index (experts j * 4 to j * 4 + 3) are named by at most 108 rows together, and those of some ep index by exactly 108. Every expert is named by some row of every device.
All inputs are finite; a program needn't handle non-finite values.
Results may differ from a plain program's by a relative error of at most 0.0014.
The roundings to bfloat16 on the way count: a program that leaves them out, or rounds other values in their place, can miss the bound.
Values may be sent and summed in bfloat16 or wider, within the bound.
No kernel may reach another device: no remote copies, remote signals or barrier semaphores. Data moves between devices by JAX's collectives and lax.ppermute only.
A program may use at most 128 MiB of HBM per device.

v0:
```python
import math
import jax
import jax.numpy as jnp
from jax import lax
from jax.sharding import PartitionSpec as P


def on_device(tokens, out_grad, indices, expert_rows, router_weight, router_bias, balance_scale):
    tok_dev = tokens.shape[0]
    chosen = indices.shape[1]
    width = tokens.shape[1]
    experts = router_weight.shape[1]
    capacity = expert_rows.shape[3]
    ep_size = lax.axis_size("ep")
    dp_size = lax.axis_size("dp")
    token_total = tok_dev * ep_size * dp_size
    expert_ids = jnp.arange(experts, dtype=jnp.int32)
    onehot = (indices[:, :, None] == expert_ids[None, None, :]).astype(jnp.float32)
    named_by = jnp.sum(onehot, axis=1)
    local_counts = jnp.sum(named_by, axis=0)
    logits = jnp.dot(tokens, router_weight, preferred_element_type=jnp.float32) + router_bias
    probability = jax.nn.softmax(logits, axis=-1)
    counts, prob_sums = lax.psum((local_counts, jnp.sum(probability, axis=0)), ("ep", "dp"))
    share_of = counts / (token_total * chosen)
    balance_loss = (experts * jnp.sum(share_of * (prob_sums / token_total))).reshape(1)
    row_ids = jnp.arange(tok_dev, dtype=jnp.int32)
    lower_mask = (row_ids[:, None] > row_ids[None, :]).astype(jnp.bfloat16)
    before = jnp.dot(lower_mask, named_by.astype(jnp.bfloat16), preferred_element_type=jnp.float32)
    slot_index = jnp.sum(onehot * before[:, None, :], axis=2).astype(jnp.int32)
    returned = lax.all_to_all(expert_rows, "ep", split_axis=2, concat_axis=1, tiled=True)
    flat_rows = returned.reshape(experts * capacity, width)
    row_index = indices * capacity + slot_index
    picked = jnp.take(flat_rows, row_index, axis=0)
    pair_dots = jnp.einsum("td,tkd->tk", out_grad, picked, preferred_element_type=jnp.float32)
    chosen_logits = jnp.take_along_axis(logits, indices, axis=1)
    mix_weight = jax.nn.softmax(chosen_logits, axis=-1)
    sel_grad = mix_weight * (pair_dots - jnp.sum(mix_weight * pair_dots, axis=1, keepdims=True))
    balance_push = balance_scale[0] * experts * share_of
    spread = probability * (
        balance_push[None, :] - jnp.sum(probability * balance_push[None, :], axis=1, keepdims=True)
    )
    logit_grad = (spread + jnp.sum(onehot * sel_grad[:, :, None], axis=1)).astype(jnp.bfloat16)
    token_grad = lax.dot_general(
        logit_grad, router_weight, (((1,), (1,)), ((), ())), preferred_element_type=jnp.float32
    ).astype(jnp.bfloat16)
    term = lax.dot_general(
        tokens, logit_grad, (((0,), (0,)), ((), ())), preferred_element_type=jnp.float32
    )
    summed = lax.psum_scatter(term, "ep", scatter_dimension=1, tiled=True)
    summed = lax.psum_scatter(summed, "dp", scatter_dimension=0, tiled=True)
    weight_grad = summed / math.sqrt(token_total)
    return (token_grad, weight_grad, balance_loss)


def solution(mesh):
    placed = (
        P(("ep", "dp"), None),
        P(("ep", "dp"), None),
        P(("ep", "dp"), None),
        P("dp", "ep", None, None, None),
        P(),
        P(),
        P(),
    )
    return jax.shard_map(
        on_device,
        mesh=mesh,
        in_specs=placed,
        out_specs=(P(("ep", "dp"), None), P("dp", "ep"), P()),
        check_vma=False,
    )
```

profile of v0, /device:TPU:0, one launch (start us, length us, event | category | flops | bytes accessed | tf_op | source)
XLA Modules:
  0.0 366.3 jit_solution(14106931418418347998)
XLA Ops:
  7.2 0.0 copy-start
  7.2 7.0 %copy.48 = bf16[1,4,8,36,2880]{4,3,1,0,2:T(8,128)(2,1)} copy(bf16[1,4,8,36,2880]{4,2,3,1,0:T(8,128)(2,1)} %param.10) | data formatting | bytes 13271040 | tf_op args[3]
  14.2 0.0 copy-start.3
  14.2 0.0 copy-start.1
  14.2 0.0 copy-start.2
  14.2 0.0 copy-start.4
  14.2 7.5 %all-to-all-start = ((bf16[1,4,8,36,2880]{4,3,1,0,2:T(8,128)(2,1)}), bf16[1,4,8,36,2880]{4,3,1,0,2:T(8,128)(2,1)}, u32[]{:S(2)}, u32[]{:S(2)}) async-start(bf16[1,4,8,36,2880]{4,3,1,0,2:T(8,128)(2,1)} %copy.48), calls=%async_computation | async-start | bytes 15073280 | tf_op jit(solution)/shard_map/all_to_all | solution.py:30
  21.7 0.0 all-reduce.3.cloned.1.call-start
  21.7 0.0 copy-done.3
  21.8 0.1 fusion.5
  21.9 0.2 convert_reduce_fusion.1
  22.1 184.7 %psum.14 = f32[32]{0:T(128)S(1)} all-reduce(f32[32]{0:T(128)S(1)} %get-tuple-element.5), channel_id=1, replica_groups=mesh['ep'=8,'dp'=4] {'ep','dp'}, use_global_device_ids=true, to_apply=%region_3.0 | all-reduce | flops 32 | bytes 256 | tf_op jit(solution)/shard_map/psum | solution.py:23
  206.8 0.1 copy.49
  206.9 0.1 reshape.45
  207.0 0.2 copy.47
  207.2 0.1 copy.45
  207.3 0.1 reshape.51
  207.4 0.0 copy-done.1
  207.4 0.0 copy-done.2
  207.4 0.0 copy-done.4
  207.4 0.5 fusion.16
  207.9 6.3 %gather_fusion.1 = f32[768]{0:T(1024)S(1)} fusion(f32[192,32]{0,1:T(8,128)S(1)} %get-tuple-element.12, s32[768]{0:T(1024)S(1)} %reshape.51), kind=kCustom, calls=%fused_computation.1 | custom fusion | bytes 12288 | tf_op jit(solution)/shard_map/jit(take_along_axis)/gather | solution.py:35
  214.3 0.1 reshape.54
  214.4 0.1 copy.46
  215.2 0.1 fusion.14
  215.4 0.0 all-to-all-done
  215.4 9.3 %reshape.41 = bf16[1152,2880]{1,0:T(8,128)(2,1)} reshape(bf16[1,8,4,1,36,2880]{5,4,2,1,3,0:T(8,128)(2,1)} %bitcast.3) | data formatting | bytes 13271040 | tf_op jit(solution)/shard_map/reshape | solution.py:31
  224.7 13.1 %gather_fusion = bf16[768,2880]{1,0:T(8,128)(2,1)} fusion(bf16[1152,2880]{1,0:T(8,128)(2,1)} %reshape.41, s32[1024]{0:T(1024)S(1)} %pad_clamp_fusion), kind=kCustom, calls=%fused_computation | custom fusion | bytes 8850432 | tf_op jit(solution)/shard_map/jit(_take)/gather | solution.py:33
  237.8 7.1 %reshape.44 = bf16[192,4,2880]{2,1,0:T(4,128)(2,1)} reshape(bf16[768,2880]{1,0:T(8,128)(2,1)} %gather_fusion) | data formatting | bytes 8847360 | tf_op jit(solution)/shard_map/jit(_take)/gather | solution.py:33
  244.9 0.0 copy-done
  244.9 9.4 %fusion = f32[192,1,4]{2,1,0:T(1,128)S(1)} fusion(bf16[192,4,2880]{2,1,0:T(4,128)(2,1)} %reshape.44, pred[192,4]{1,0:T(8,128)(4,1)S(1)} %copy.47, bf16[192,2880,1]{1,0,2:T(8,128)(2,1)S(1)} %bitcast.30), kind=kOutput, calls=%fused_computation.2 | convolution fusion | flops 6635520 | bytes 5533440 | tf_op jit(solution)/shard_map/td,tkd->tk/dot_general | solution.py:34
  254.3 0.1 copy.51
  254.5 0.1 add_convert_fusion
  254.6 1.1 convolution_bitcast_fusion
  255.7 0.0 all-reduce.3.cloned.1.call-update
  255.7 0.0 reduce-scatter.4.cloned.1.call-start
  255.7 39.3 %psum.15 = f32[32]{0:T(128)S(1)} all-reduce(f32[32]{0:T(128)S(1)} %get-tuple-element.3), channel_id=1, replica_groups=mesh['ep'=8,'dp'=4] {'ep','dp'}, use_global_device_ids=true, to_apply=%region_14.15 | all-reduce | flops 32 | bytes 256 | tf_op jit(solution)/shard_map/psum | solution.py:23
  295.0 0.0 copy-done.5
  295.0 0.6 dynamic-slice
  296.3 0.6 multiply_reduce_fusion.1
  297.5 29.8 %all-reduce.3.cloned.1.call-done = f32[2880,32]{0,1:T(8,128)} async-done(((f32[2880,32]{0,1:T(8,128)}), f32[2880,32]{0,1:T(8,128)}) %all-reduce.3.cloned.1.call-update) | async-done | bytes 368656
  327.3 0.9 constant_dynamic-slice_fusion
  328.2 1.6 copy.52
  329.8 0.0 reduce-scatter.4.cloned.1.call-update
  329.9 1.5 convolution_convert_fusion
  331.4 25.2 %reduce-scatter.4.cloned.1.call-done = f32[720,4]{1,0:T(8,128)} async-done(((f32[2880,4]{1,0:T(8,128)}), f32[720,4]{1,0:T(8,128)}) %reduce-scatter.4.cloned.1.call-update) | async-done | bytes 11536
  356.6 1.1 copy.53
  357.7 0.6 broadcast_multiply_fusion
  (12 shorter events, 0.2 us)
Async XLA Ops:
  7.2 237.8 %copy-start = (bf16[192,2880]{1,0:T(8,128)(2,1)S(1)}, bf16[192,2880]{1,0:T(8,128)(2,1)}, u32[]{:S(2)}) copy-start(bf16[192,2880]{1,0:T(8,128)(2,1)} %param.8) | copy-start | bytes 3317764
  14.2 7.5 %copy-start.3 = (s32[192,4]{0,1:T(4,128)S(1)}, s32[192,4]{0,1:T(4,128)}, u32[]{:S(2)}) copy-start(s32[192,4]{0,1:T(4,128)} %param.9) | copy-start | bytes 9220
  14.2 193.2 %copy-start.1 = (bf16[192,2880]{1,0:T(8,128)(2,1)S(1)}, bf16[192,2880]{1,0:T(8,128)(2,1)}, u32[]{:S(2)}) copy-start(bf16[192,2880]{1,0:T(8,128)(2,1)} %param.7) | copy-start | bytes 3317764
  14.2 193.2 %copy-start.2 = (bf16[2880,32]{0,1:T(8,128)(2,1)S(1)}, bf16[2880,32]{0,1:T(8,128)(2,1)}, u32[]{:S(2)}) copy-start(bf16[2880,32]{0,1:T(8,128)(2,1)} %param.11) | copy-start | bytes 552964
  14.2 193.2 %copy-start.4 = (f32[32]{0:T(128)S(1)}, f32[32]{0:T(128)}, u32[]{:S(2)}) copy-start(f32[32]{0:T(128)} %param.12) | copy-start | bytes 388
  14.2 201.1 %all-to-all-start = ((bf16[1,4,8,36,2880]{4,3,1,0,2:T(8,128)(2,1)}), bf16[1,4,8,36,2880]{4,3,1,0,2:T(8,128)(2,1)}, u32[]{:S(2)}, u32[]{:S(2)}) async-start(bf16[1,4,8,36,2880]{4,3,1,0,2:T(8,128)(2,1)} %copy.48), calls=%async_computation | async-start | bytes 15073280 | tf_op jit(solution)/shard_map/all_to_all | solution.py:30
  21.7 305.6 %all-reduce.3.cloned.1.call-start = ((), (), s32[]{:S(2)}) async-start(), calls=%async_computation.3 | async-start | bytes 753664
  244.9 50.1 %copy-start.5 = (u32[32]{0:T(128)S(1)}, u32[32]{0:T(128)}, u32[]{:S(2)}) copy-start(u32[32]{0:T(128)} %constant.70) | copy-start | bytes 388
  255.7 100.9 %reduce-scatter.4.cloned.1.call-start = ((), (), s32[]{:S(2)}) async-start(), calls=%async_computation.2 | async-start | bytes 1843200
Sparse Core Ops, SparseCore 0:
  255.8 71.4 all-reduce.2
  330.0 26.5 reduce-scatter.3
where the time goes:
time: 367 us; the launch traced here: 366 us
  blocking collectives  224 us (61%)
  waiting for transfers between devices  55.1 us (15%)
  local copies, waits for them, and re-layouts  48.1 us (13%)
  between operations  17.3 us (5%)
  matrix products  12.6 us (3%)
  starting transfers between devices  7.53 us (2%)
    psum x2, blocking collectives, on_device(): lax.psum((local_counts, jnp.sum(probability, axis=0)), ('ep', 'dp'))  224 us
    unnamed x4, waiting for transfers between devices  55.1 us
    gather x2, local copies, waits for them, and re-layouts, on_device(): picked = jnp.take(flat_rows, row_index, axis=0)  20.2 us
    unnamed x17, local copies, waits for them, and re-layouts  11.3 us
    dot_general x1, matrix products, on_device(): jnp.einsum('td,tkd->tk', out_grad, picked, preferred_element_type=jnp.flo...  9.4 us
    reshape x1, local copies, waits for them, and re-layouts, on_device(): flat_rows = returned.reshape(experts * capacity, width)  9.32 us
    all_to_all x1, starting transfers between devices, on_device(): lax.all_to_all(expert_rows, 'ep', split_axis=2, concat_axis=1, tiled=True)  7.45 us
  transfers between devices with their start and end apart: 3, of which 2 were waited for; matrix products, arithmetic and copies ran while one was open for 3% of the time, Pallas kernels for 0%

commit v1 on v0

--- a/solution.py
+++ b/solution.py
@@ -20,7 +20,7 @@
     local_counts = jnp.sum(named_by, axis=0)
     logits = jnp.dot(tokens, router_weight, preferred_element_type=jnp.float32) + router_bias
     probability = jax.nn.softmax(logits, axis=-1)
-    counts, prob_sums = lax.psum((local_counts, jnp.sum(probability, axis=0)), ("ep", "dp"))
+    counts, prob_sums = lax.psum(lax.psum((local_counts, jnp.sum(probability, axis=0)), "ep"), "dp")
     share_of = counts / (token_total * chosen)
     balance_loss = (experts * jnp.sum(share_of * (prob_sums / token_total))).reshape(1)
     row_ids = jnp.arange(tok_dev, dtype=jnp.int32)

time: 367 us -> 352 us (0.959)
  blocking collectives: 224 us -> 185 us
  waiting for transfers between devices: 55.1 us -> 78.8 us
    psum x2 -> x4, blocking collectives: 224 us -> 185 us  [the longest x2 173 us: on_device(): lax.psum((local_counts, jnp.sum(probability, axis=0)), 'ep')]
    unnamed x4, waiting for transfers between devices: 55.1 us -> 68 us
    all_to_all x1, waiting for transfers between devices: 0.01 us -> 10.8 us  [on_device(): lax.all_to_all(expert_rows, 'ep', split_axis=2, concat_axis=1, tiled=True)]
  transfers between devices with their start and end apart: 3 -> 3, of which waited for: 2 -> 3; matrix products, arithmetic and copies ran while one was open for 3% -> 3% of each run, Pallas kernels for 0% -> 0%
where the time goes in v1:
time: 352 us; the launch traced here: 351 us
  blocking collectives  185 us (53%)
  waiting for transfers between devices  78.8 us (22%)
  local copies, waits for them, and re-layouts  48.1 us (14%)
  between operations  17.3 us (5%)
  matrix products  12.6 us (4%)
  starting transfers between devices  7.53 us (2%)
    psum x2, blocking collectives, on_device(): lax.psum((local_counts, jnp.sum(probability, axis=0)), 'ep')  173 us
    unnamed x4, waiting for transfers between devices  68 us
    gather x2, local copies, waits for them, and re-layouts, on_device(): picked = jnp.take(flat_rows, row_index, axis=0)  20.2 us
    psum x2, blocking collectives, on_device(): lax.psum(lax.psum((local_counts, jnp.sum(probability, axis=0)), 'ep'), 'dp')  12.1 us
    unnamed x17, local copies, waits for them, and re-layouts  11.3 us
    all_to_all x1, waiting for transfers between devices, on_device(): lax.all_to_all(expert_rows, 'ep', split_axis=2, concat_axis=1, tiled=True)  10.8 us
    dot_general x1, matrix products, on_device(): jnp.einsum('td,tkd->tk', out_grad, picked, preferred_element_type=jnp.flo...  9.4 us
    reshape x1, local copies, waits for them, and re-layouts, on_device(): flat_rows = returned.reshape(experts * capacity, width)  9.31 us
  transfers between devices with their start and end apart: 3, of which 3 were waited for; matrix products, arithmetic and copies ran while one was open for 3% of the time, Pallas kernels for 0%

profile of v1, /device:TPU:0, one launch (start us, length us, event | category | flops | bytes accessed | tf_op | source)
XLA Modules:
  0.0 351.1 jit_solution(17235843222115780855)
XLA Ops:
  7.2 0.0 copy-start
  7.2 7.0 %copy.48 = bf16[1,4,8,36,2880]{4,3,1,0,2:T(8,128)(2,1)} copy(bf16[1,4,8,36,2880]{4,2,3,1,0:T(8,128)(2,1)} %param.10) | data formatting | bytes 13271040 | tf_op args[3]
  14.2 0.0 copy-start.3
  14.2 0.0 copy-start.1
  14.2 7.5 %all-to-all-start = ((bf16[1,4,8,36,2880]{4,3,1,0,2:T(8,128)(2,1)}), bf16[1,4,8,36,2880]{4,3,1,0,2:T(8,128)(2,1)}, u32[]{:S(2)}, u32[]{:S(2)}) async-start(bf16[1,4,8,36,2880]{4,3,1,0,2:T(8,128)(2,1)} %copy.48), calls=%async_computation | async-start | bytes 15073280 | tf_op jit(solution)/shard_map/all_to_all | solution.py:30
  21.7 0.0 all-reduce.3.cloned.1.call-start
  21.7 0.0 copy-done.3
  21.8 0.1 fusion.5
  21.9 0.2 convert_reduce_fusion.1
  22.1 0.1 copy.49
  22.2 0.1 reshape.45
  22.3 0.2 copy.47
  22.5 0.1 copy.45
  22.6 0.1 reshape.51
  22.8 0.0 copy-done.1
  22.8 0.0 copy-done.2
  22.8 0.0 copy-done.4
  22.8 0.5 fusion.16
  23.3 6.3 %gather_fusion.1 = f32[768]{0:T(1024)S(1)} fusion(f32[192,32]{0,1:T(8,128)S(1)} %get-tuple-element.12, s32[768]{0:T(1024)S(1)} %reshape.51), kind=kCustom, calls=%fused_computation.1 | custom fusion | bytes 12288 | tf_op jit(solution)/shard_map/jit(take_along_axis)/gather | solution.py:35
  29.6 0.1 reshape.54
  29.7 0.1 copy.46
  30.5 139.1 %psum.28 = f32[32]{0:T(128)S(1)} all-reduce(f32[32]{0:T(128)S(1)} %get-tuple-element.5), channel_id=1, replica_groups=mesh['ep'=8,'dp'=4] {'ep'}, use_global_device_ids=true, to_apply=%region_3.0 | all-reduce | flops 32 | bytes 256 | tf_op jit(solution)/shard_map/psum | solution.py:23
  169.6 6.0 %psum.29 = f32[32]{0:T(128)S(1)} all-reduce(f32[32]{0:T(128)S(1)} %psum.28), channel_id=1, replica_groups=mesh['ep'=8,'dp'=4] {'dp'}, use_global_device_ids=true, to_apply=%region_4.0 | all-reduce | flops 32 | bytes 256 | tf_op jit(solution)/shard_map/psum | solution.py:23
  175.8 0.1 fusion.14
  175.9 10.8 %all-to-all-done = bf16[1,4,8,36,2880]{4,3,1,0,2:T(8,128)(2,1)} async-done(((bf16[1,4,8,36,2880]{4,3,1,0,2:T(8,128)(2,1)}), bf16[1,4,8,36,2880]{4,3,1,0,2:T(8,128)(2,1)}, u32[]{:S(2)}, u32[]{:S(2)}) %all-to-all-start) | async-done | bytes 6635552 | tf_op jit(solution)/shard_map/all_to_all | solution.py:30
  186.7 9.3 %reshape.41 = bf16[1152,2880]{1,0:T(8,128)(2,1)} reshape(bf16[1,8,4,1,36,2880]{5,4,2,1,3,0:T(8,128)(2,1)} %bitcast.3) | data formatting | bytes 13271040 | tf_op jit(solution)/shard_map/reshape | solution.py:31
  196.0 13.1 %gather_fusion = bf16[768,2880]{1,0:T(8,128)(2,1)} fusion(bf16[1152,2880]{1,0:T(8,128)(2,1)} %reshape.41, s32[1024]{0:T(1024)S(1)} %pad_clamp_fusion), kind=kCustom, calls=%fused_computation | custom fusion | bytes 8850432 | tf_op jit(solution)/shard_map/jit(_take)/gather | solution.py:33
  209.1 7.1 %reshape.44 = bf16[192,4,2880]{2,1,0:T(4,128)(2,1)} reshape(bf16[768,2880]{1,0:T(8,128)(2,1)} %gather_fusion) | data formatting | bytes 8847360 | tf_op jit(solution)/shard_map/jit(_take)/gather | solution.py:33
  216.2 0.0 copy-done
  216.2 9.4 %fusion = f32[192,1,4]{2,1,0:T(1,128)S(1)} fusion(bf16[192,4,2880]{2,1,0:T(4,128)(2,1)} %reshape.44, pred[192,4]{1,0:T(8,128)(4,1)S(1)} %copy.47, bf16[192,2880,1]{1,0,2:T(8,128)(2,1)S(1)} %bitcast.30), kind=kOutput, calls=%fused_computation.2 | convolution fusion | flops 6635520 | bytes 5533440 | tf_op jit(solution)/shard_map/td,tkd->tk/dot_general | solution.py:34
  225.6 0.1 copy.51
  225.8 0.1 add_convert_fusion
  225.9 1.1 convolution_bitcast_fusion
  227.0 0.0 all-reduce.3.cloned.1.call-update
  227.0 0.0 reduce-scatter.4.cloned.1.call-start
  227.0 0.0 copy-done.5
  227.1 0.6 dynamic-slice
  228.3 33.8 %psum.30 = f32[32]{0:T(128)S(1)} all-reduce(f32[32]{0:T(128)S(1)} %get-tuple-element.3), channel_id=1, replica_groups=mesh['ep'=8,'dp'=4] {'ep'}, use_global_device_ids=true, to_apply=%region_15.16 | all-reduce | flops 32 | bytes 256 | tf_op jit(solution)/shard_map/psum | solution.py:23
  262.1 6.0 %psum.31 = f32[32]{0:T(128)S(1)} all-reduce(f32[32]{0:T(128)S(1)} %psum.30), channel_id=1, replica_groups=mesh['ep'=8,'dp'=4] {'dp'}, use_global_device_ids=true, to_apply=%region_16.17 | all-reduce | flops 32 | bytes 256 | tf_op jit(solution)/shard_map/psum | solution.py:23
  268.1 0.6 multiply_reduce_fusion.1
  269.4 42.7 %all-reduce.3.cloned.1.call-done = f32[2880,32]{0,1:T(8,128)} async-done(((f32[2880,32]{0,1:T(8,128)}), f32[2880,32]{0,1:T(8,128)}) %all-reduce.3.cloned.1.call-update) | async-done | bytes 368656
  312.1 0.9 constant_dynamic-slice_fusion
  313.0 1.6 copy.52
  314.6 0.0 reduce-scatter.4.cloned.1.call-update
  314.6 1.5 convolution_convert_fusion
  316.1 25.2 %reduce-scatter.4.cloned.1.call-done = f32[720,4]{1,0:T(8,128)} async-done(((f32[2880,4]{1,0:T(8,128)}), f32[720,4]{1,0:T(8,128)}) %reduce-scatter.4.cloned.1.call-update) | async-done | bytes 11536
  341.4 1.1 copy.53
  342.5 0.6 broadcast_multiply_fusion
  (14 shorter events, 0.2 us)
Async XLA Ops:
  7.2 209.1 %copy-start = (bf16[192,2880]{1,0:T(8,128)(2,1)S(1)}, bf16[192,2880]{1,0:T(8,128)(2,1)}, u32[]{:S(2)}) copy-start(bf16[192,2880]{1,0:T(8,128)(2,1)} %param.8) | copy-start | bytes 3317764
  14.2 7.5 %copy-start.3 = (s32[192,4]{0,1:T(4,128)S(1)}, s32[192,4]{0,1:T(4,128)}, u32[]{:S(2)}) copy-start(s32[192,4]{0,1:T(4,128)} %param.9) | copy-start | bytes 9220
  14.2 8.5 %copy-start.1 = (bf16[192,2880]{1,0:T(8,128)(2,1)S(1)}, bf16[192,2880]{1,0:T(8,128)(2,1)}, u32[]{:S(2)}) copy-start(bf16[192,2880]{1,0:T(8,128)(2,1)} %param.7) | copy-start | bytes 3317764
  14.2 8.5 %copy-start.2 = (bf16[2880,32]{0,1:T(8,128)(2,1)S(1)}, bf16[2880,32]{0,1:T(8,128)(2,1)}, u32[]{:S(2)}) copy-start(bf16[2880,32]{0,1:T(8,128)(2,1)} %param.11) | copy-start | bytes 552964
  14.2 8.5 %copy-start.4 = (f32[32]{0:T(128)S(1)}, f32[32]{0:T(128)}, u32[]{:S(2)}) copy-start(f32[32]{0:T(128)} %param.12) | copy-start | bytes 388
  14.2 172.5 %all-to-all-start = ((bf16[1,4,8,36,2880]{4,3,1,0,2:T(8,128)(2,1)}), bf16[1,4,8,36,2880]{4,3,1,0,2:T(8,128)(2,1)}, u32[]{:S(2)}, u32[]{:S(2)}) async-start(bf16[1,4,8,36,2880]{4,3,1,0,2:T(8,128)(2,1)} %copy.48), calls=%async_computation | async-start | bytes 15073280 | tf_op jit(solution)/shard_map/all_to_all | solution.py:30
  21.7 290.4 %all-reduce.3.cloned.1.call-start = ((), (), s32[]{:S(2)}) async-start(), calls=%async_computation.3 | async-start | bytes 753664
  216.2 10.8 %copy-start.5 = (u32[32]{0:T(128)S(1)}, u32[32]{0:T(128)}, u32[]{:S(2)}) copy-start(u32[32]{0:T(128)} %constant.70) | copy-start | bytes 388
  227.0 114.4 %reduce-scatter.4.cloned.1.call-start = ((), (), s32[]{:S(2)}) async-start(), calls=%async_computation.2 | async-start | bytes 1843200
Sparse Core Ops, SparseCore 0:
  227.1 84.9 all-reduce.2
  314.8 26.5 reduce-scatter.3
